TPU v7x, 32 devices: a whole 2x2x4 slice. The times are simulated.
32 devices in a mesh: ev: 2 (over core), own: 16 (over z, y, x).
Axes of the slice: x: 2, y: 2, z: 4, core: 2. Of those that a mesh axis runs over, the one named last changes fastest.
Arguments:
- ground_up: bfloat16 [8192, 4096], P('own', 'ev'), parts along dimension 1, may hold values from 0.049804688 to 2
- item_site: int32 [8192], P('own'), may hold values from 0 to 127
- item_profile: int32 [8192], P('own'), may hold values from 0 to 127
- site_owner: int32 [2048, 1], P('own'), may hold values from 0 to 15; in each aligned block of 128 rows (0 to 127, 128 to 255, ...) at most 16 rows name the same one
- site_slot: int32 [2048], P('own'), may hold values from 0 to 63
- site_profile: int32 [2048], P('own'), may hold values from 0 to 127
- policy_owner: int32 [1024, 1], P('own'), may hold values from 0 to 15; in each aligned block of 64 rows (0 to 63, 64 to 127, ...) at most 12 rows name the same one
- policy_slot: int32 [1024], P('own'), may hold values from 0 to 1
- policy_profile: int32 [1024], P('own'), may hold values from 0 to 127
- program_profile: int32 [32], P('own'), may hold values from 0 to 127
- term_table: float32 [4, 3, 128], replicated, may hold values from 0 to 90, as said below
Outputs:
- policy_loss: bfloat16 [1024, 4096], P('own', 'ev'), parts along dimension 1
- program_loss: float32 [32, 4096], P('own', 'ev'), parts along dimension 1
There are 2 independent parts, one for each index of `ev`. A program takes and returns all parts, laid end to end along the dimension named above; an argument that names none is the same for every part. Nothing has to cross between parts.
Inputs may be any that keep to these rules, and one draw needn't show every extreme that they name: `site_owner`: among the 128 sites of one owner, no owner of policies appears more than 16 times; some owner appears exactly 16 times in some owner's sites. `policy_owner`: among the 64 policies of one owner, no owner of programs appears more than 12 times; some owner appears exactly 12 times in some owner's policies. `term_table`: deductibles are 0 or more, limits positive, shares between 0.5 and 1.
All inputs are finite; a program needn't handle non-finite values.
Results may differ from a plain program's by a relative error of at most 0.0051.
Values may be sent and summed in bfloat16 or wider, within the bound.
A program may use at most 64 MiB of HBM per device.

v0:
```python
import functools

import jax
import jax.numpy as jnp
from jax import lax
from jax.experimental import pallas as pl
from jax.experimental.pallas import tpu as pltpu
from jax.sharding import PartitionSpec as P

LANES = 128
SMALL = 10
f32 = jnp.float32
bf16 = jnp.bfloat16


def terms(x, deduct, ceiling, portion):
    return portion * jnp.minimum(jnp.maximum(x - deduct, 0.0), ceiling)


def across(me, k, n):
    d, bit = 0, 1
    while bit < n:
        d = d + bit * lax.rem(lax.div(me, bit) + (k // bit) % 2, 2)
        bit *= 2
    return d


def route(n):
    return [*range(1, n)]


def kernel(
    n,
    pol,
    prog,
    ground,
    *refs,
):
    small_in, refs = refs[:SMALL], refs[SMALL:]
    policy_out, program_out = refs[:2]
    small, refs = refs[2 : 2 + SMALL], refs[2 + SMALL :]
    (
        chunks,
        ids,
        square,
        item_terms,
        site_terms,
        policy_terms,
        program_terms,
        grouping,
        meta,
        send,
        recv,
        acc,
        losses,
        program_send,
        marks,
        picks,
        small_sem,
        load_sem,
        meta_ss,
        meta_rs,
        site_ss,
        site_rs,
        pol_ss,
        pol_rs,
        prog_ss,
        prog_rs,
    ) = refs
    me = lax.axis_index("own")
    groups = n // 2
    mine = me // 2
    half = groups // 2
    items = ground.shape[0]
    blocks = items // LANES
    sites = send.shape[1]
    width = send.shape[2]
    wide = 2 * width

    barrier = pltpu.get_barrier_semaphore()

    def greet(k, c):
        pl.semaphore_signal(barrier, inc=1, device_id={"own": lax.rem(me + k, n)})
        return c

    lax.fori_loop(1, n, greet, 0)

    def fetch(i):
        return pltpu.make_async_copy(small_in[i], small[i], small_sem.at[i])

    for i in range(SMALL):
        fetch(i).start()

    def load(i):
        g = lax.rem(mine + half + i, groups)
        return pltpu.make_async_copy(
            ground.at[:, pl.ds(pl.multiple_of(g * wide, wide), wide)],
            chunks.at[i],
            load_sem.at[i],
        )

    def start_load(i, c):
        load(i).start()
        return c

    lax.fori_loop(0, groups, start_load, 0)
    (
        item_site,
        item_profile,
        site_owner,
        site_slot,
        site_profile,
        policy_owner,
        policy_slot,
        policy_profile,
        program_profile,
        table,
    ) = small
    for i in range(SMALL):
        fetch(i).wait()

    square[...] = jnp.zeros_like(square)
    for t in range(3):
        square[4 * t : 4 * t + 4, :] = table[t]
    columns = square[...].T
    rows_iota = lax.broadcasted_iota(jnp.int32, (LANES, LANES), 0)

    def look(profile_row, level):
        pick = rows_iota == profile_row
        return [
            jnp.sum(
                jnp.where(pick, columns[:, 4 * t + level : 4 * t + level + 1], 0.0),
                axis=0,
                keepdims=True,
            )
            for t in range(3)
        ]

    ids[...] = jnp.zeros_like(ids)
    ids[0:1, 0:pol] = policy_profile[...]
    ids[0:1, pol : 2 * pol] = policy_owner[...] * prog + policy_slot[...]
    ids[1:2, 0:prog] = program_profile[...]
    meta[me] = jnp.concatenate([site_owner[...] * pol + site_slot[...], ids[0:1, :]], axis=0)

    for b in range(blocks):
        grouping[:, b * LANES : (b + 1) * LANES] = (rows_iota == item_site[b : b + 1, :]).astype(bf16)
        for t, row in enumerate(look(item_profile[b : b + 1, :], 0)):
            square[3 * b + t : 3 * b + t + 1, :] = row
    for t, row in enumerate(look(site_profile[...], 1)):
        square[3 * blocks + t : 3 * blocks + t + 1, :] = row
    for t, row in enumerate(look(ids[1:2, :], 3)):
        square[3 * blocks + 3 + t : 3 * blocks + 4 + t, :] = row
    flipped = square[...].T
    for t in range(3):
        for b in range(blocks):
            item_terms[t, b * LANES : (b + 1) * LANES, :] = jnp.broadcast_to(
                flipped[:, 3 * b + t : 3 * b + t + 1], (LANES, LANES)
            )
        program_terms[t] = jnp.broadcast_to(
            flipped[0:prog, 3 * blocks + 3 + t : 3 * blocks + 4 + t], (prog, LANES)
        )
        site_terms[t] = jnp.broadcast_to(
            flipped[:, 3 * blocks + t : 3 * blocks + t + 1], (LANES, LANES)
        )

    def meta_copy(d, s):
        return pltpu.make_async_remote_copy(
            meta.at[s], meta.at[s], meta_ss.at[d], meta_rs.at[s], device_id={"own": d}
        )

    def site_copy(d, s):
        return pltpu.make_async_remote_copy(
            send.at[d], recv.at[s], site_ss.at[d], site_rs.at[s], device_id={"own": d}
        )

    def policy_copy(d, s):
        return pltpu.make_async_remote_copy(
            losses.at[pl.ds(pl.multiple_of(d * pol, pol), pol), :],
            policy_out.at[:, pl.ds(pl.multiple_of(s * width, width), width)],
            pol_ss.at[d],
            pol_rs.at[s],
            device_id={"own": d},
        )

    def program_copy(d, s):
        return pltpu.make_async_remote_copy(
            program_send.at[d],
            program_out.at[:, pl.ds(pl.multiple_of(s * width, width), width)],
            prog_ss.at[d],
            prog_rs.at[s],
            device_id={"own": d},
        )

    def others(fn):
        def step(k, c):
            fn(lax.rem(me + k, n))
            return c

        lax.fori_loop(1, n, step, 0)

    def sites_step(i, c):
        load(i).wait()
        g = lax.rem(mine + half + i, groups)
        spread = [jnp.concatenate([item_terms[t]] * (wide // LANES), axis=1) for t in range(3)]
        covered = terms(chunks[i].astype(f32), *spread).astype(bf16)
        gross = jnp.dot(grouping[...], covered, preferred_element_type=f32)
        site_spread = [jnp.concatenate([site_terms[t]] * (wide // LANES), axis=1) for t in range(3)]
        net = terms(gross, *site_spread).astype(bf16)
        for j in range(2):
            d = 2 * g + j
            piece = net[:, j * width : (j + 1) * width]

            @pl.when(d == me)
            def _():
                recv[me] = piece

            @pl.when(d != me)
            def _():
                send[d] = piece

        return c

    lax.fori_loop(0, groups, sites_step, 0)

    pl.semaphore_wait(barrier, n - 1)

    others(lambda d: meta_copy(d, me).start())

    for k in route(n):
        d = across(me, k, n)
        site_copy(d, me).start()

    others(lambda s: meta_copy(me, s).wait_recv())

    for o in range(n):
        for t, row in enumerate(look(meta[o][1:2, :], 2)):
            square[3 * o + t : 3 * o + t + 1, :] = row
    turned = square[...].T
    for o in range(n):
        for t in range(3):
            lane = 3 * o + t
            policy_terms[t, o * pol : (o + 1) * pol, :] = jnp.broadcast_to(
                turned[0:pol, lane : lane + 1], (pol, LANES)
            )

    policy_iota = lax.broadcasted_iota(jnp.int32, (n * pol, sites), 0)
    program_iota = lax.broadcasted_iota(jnp.int32, (n * prog, pol), 0)
    marks[...] = jnp.concatenate(
        [(program_iota == meta[o][1:2, pol : 2 * pol]).astype(bf16) for o in range(n)], axis=1
    )
    for k in range(groups):
        g = across(mine, k, groups)
        picks[k] = jnp.concatenate(
            [(policy_iota == meta[2 * g + j][0:1, :]).astype(bf16) for j in range(2)], axis=1
        )
    acc[...] = jnp.zeros_like(acc)

    for k in range(groups):
        g = across(mine, k, groups)
        for j in range(2):
            s = 2 * g + j

            @pl.when(s != me)
            def _():
                site_copy(me, s).wait_recv()

        values = recv[pl.ds(2 * g, 2)].reshape(2 * sites, width)
        acc[...] += jnp.dot(picks[k], values, preferred_element_type=f32)

    for k in route(n) + [0]:
        d = across(me, k, n)
        at = pl.ds(pl.multiple_of(d * pol, pol), pol)
        spread = [
            jnp.concatenate([policy_terms[t, at, :]] * (width // LANES), axis=1) for t in range(3)
        ]
        losses[at, :] = terms(acc[at, :], *spread).astype(bf16)
        if k:
            policy_copy(d, me).start()
    own_policy = pltpu.make_async_copy(
        losses.at[pl.ds(pl.multiple_of(me * pol, pol), pol), :],
        policy_out.at[:, pl.ds(pl.multiple_of(me * width, width), width)],
        pol_rs.at[me],
    )
    own_policy.start()

    program_gross = jnp.dot(marks[...], losses[...], preferred_element_type=f32)
    for o in range(n):
        program_send[o] = program_gross[o * prog : (o + 1) * prog, :]
    for k in route(n):
        program_copy(across(me, k, n), me).start()
    own_program = pltpu.make_async_copy(
        program_send.at[me],
        program_out.at[:, pl.ds(pl.multiple_of(me * width, width), width)],
        prog_rs.at[me],
    )
    own_program.start()

    def finish(d):
        meta_copy(d, me).wait_send()
        site_copy(d, me).wait_send()
        policy_copy(d, me).wait_send()
        program_copy(d, me).wait_send()
        policy_copy(me, d).wait_recv()
        program_copy(me, d).wait_recv()

    others(finish)
    own_policy.wait()
    own_program.wait()
    spread = [jnp.concatenate([program_terms[t]] * (program_out.shape[1] // LANES), axis=1) for t in range(3)]
    program_out[...] = terms(program_out[...], *spread)


def exchange(
    ground_up,
    item_site,
    item_profile,
    site_owner,
    site_slot,
    site_profile,
    policy_owner,
    policy_slot,
    policy_profile,
    program_profile,
    term_table,
):
    n = lax.axis_size("own")
    items, cols = ground_up.shape
    sites = site_profile.shape[0]
    pol = policy_profile.shape[0]
    prog = program_profile.shape[0]
    width = cols // n

    def row(v):
        return v.reshape(-1, min(v.size, LANES))

    inputs = [
        row(v)
        for v in (
            item_site,
            item_profile,
            site_owner,
            site_slot,
            site_profile,
            policy_owner,
            policy_slot,
            policy_profile,
            program_profile,
        )
    ] + [term_table.transpose(1, 0, 2)]
    vmemspec = pl.BlockSpec(memory_space=pltpu.VMEM)
    anyspec = pl.BlockSpec(memory_space=pl.ANY)
    dma = pltpu.SemaphoreType.DMA
    return pl.pallas_call(
        functools.partial(kernel, n, pol, prog),
        out_shape=(
            pltpu.VMEM((pol, cols), bf16),
            pltpu.VMEM((prog, cols), f32),
        ),
        in_specs=[anyspec] * (1 + SMALL),
        out_specs=(vmemspec, vmemspec),
        scratch_shapes=[pltpu.VMEM(v.shape, v.dtype) for v in inputs]
        + [
            pltpu.VMEM((n // 2, items, 2 * width), bf16),
            pltpu.VMEM((8, LANES), jnp.int32),
            pltpu.VMEM((LANES, LANES), f32),
            pltpu.VMEM((3, items, LANES), f32),
            pltpu.VMEM((3, sites, LANES), f32),
            pltpu.VMEM((3, n * pol, LANES), f32),
            pltpu.VMEM((3, prog, LANES), f32),
            pltpu.VMEM((sites, items), bf16),
            pltpu.VMEM((n, 2, LANES), jnp.int32),
            pltpu.VMEM((n, sites, width), bf16),
            pltpu.VMEM((n, sites, width), bf16),
            pltpu.VMEM((n * pol, width), f32),
            pltpu.VMEM((n * pol, width), bf16),
            pltpu.VMEM((n, prog, width), f32),
            pltpu.VMEM((n * prog, n * pol), bf16),
            pltpu.VMEM((n // 2, n * pol, 2 * sites), bf16),
            dma((SMALL,)),
            dma((n // 2,)),
        ]
        + [dma((n,))] * 8,
        compiler_params=pltpu.CompilerParams(collective_id=0, has_side_effects=True),
        name="loss_terms",
    )(ground_up, *inputs)


def apply_terms(gross_loss, terms_table, tier_index, profile):
    profile_iota = jnp.arange(terms_table.shape[2], dtype=jnp.int32)
    picker = profile[:, None] == profile_iota[None, :]
    deduct = jnp.sum(jnp.where(picker, terms_table[tier_index, 0][None, :], 0.0), axis=1)[:, None]
    ceiling = jnp.sum(jnp.where(picker, terms_table[tier_index, 1][None, :], 0.0), axis=1)[:, None]
    portion = jnp.sum(jnp.where(picker, terms_table[tier_index, 2][None, :], 0.0), axis=1)[:, None]
    return portion * jnp.minimum(jnp.maximum(gross_loss - deduct, 0.0), ceiling)


def pack_rows(values, target_dev, inner_slot, owners, capacity):
    member = (target_dev[:, None] == jnp.arange(owners, dtype=jnp.int32)[None, :]).astype(jnp.int32)
    before = jnp.cumsum(member, axis=0) - member
    position = jnp.sum(before * member, axis=1)
    target = target_dev * capacity + position
    placer = jnp.arange(owners * capacity, dtype=jnp.int32)[:, None] == target[None, :]
    packed = jnp.dot(
        placer.astype(jnp.bfloat16), values, preferred_element_type=jnp.float32
    ).astype(jnp.bfloat16)
    labels = jnp.sum(jnp.where(placer, (inner_slot + 1)[None, :], 0), axis=1) - 1
    return (
        packed.reshape(owners, capacity, values.shape[1]),
        labels.astype(jnp.bfloat16).reshape(owners, capacity),
    )


def sum_rows(received, labels, slot_count):
    flattened = received.reshape(-1, received.shape[2])
    slot_marks = labels.reshape(-1).astype(jnp.int32)
    picker = (jnp.arange(slot_count, dtype=jnp.int32)[:, None] == slot_marks[None, :]).astype(
        jnp.bfloat16
    )
    return jnp.dot(picker, flattened, preferred_element_type=jnp.float32)


def shards(
    ground_up,
    item_site,
    item_profile,
    site_owner,
    site_slot,
    site_profile,
    policy_owner,
    policy_slot,
    policy_profile,
    program_profile,
    term_table,
):
    owners = lax.axis_size("own")
    covered = apply_terms(ground_up.astype(jnp.float32), term_table, 0, item_profile).astype(
        jnp.bfloat16
    )
    site_total = site_profile.shape[0]
    grouping = (jnp.arange(site_total, dtype=jnp.int32)[:, None] == item_site[None, :]).astype(
        jnp.bfloat16
    )
    site_gross = jnp.dot(grouping, covered, preferred_element_type=jnp.float32)
    site_net = apply_terms(site_gross, term_table, 1, site_profile).astype(jnp.bfloat16)
    capacity = 2 * site_total // owners
    packed, labels = pack_rows(site_net, site_owner[:, 0], site_slot, owners, capacity)
    arrived, arrived_labels = (
        lax.all_to_all(packed, "own", split_axis=0, concat_axis=0, tiled=True),
        lax.all_to_all(labels, "own", split_axis=0, concat_axis=0, tiled=True),
    )
    policy_total = policy_profile.shape[0]
    policy_gross = sum_rows(arrived, arrived_labels, policy_total)
    policy_loss = apply_terms(policy_gross, term_table, 2, policy_profile).astype(jnp.bfloat16)
    program_total = program_profile.shape[0]
    program_capacity = 3 * policy_total // owners
    sent_rows, sent_labels = pack_rows(
        policy_loss, policy_owner[:, 0], policy_slot, owners, program_capacity
    )
    got_rows, got_labels = (
        lax.all_to_all(sent_rows, "own", split_axis=0, concat_axis=0, tiled=True),
        lax.all_to_all(sent_labels, "own", split_axis=0, concat_axis=0, tiled=True),
    )
    program_gross = sum_rows(got_rows, got_labels, program_total)
    program_loss = apply_terms(program_gross, term_table, 3, program_profile)
    return (policy_loss, program_loss)


def solution(mesh):
    placed = (
        P("own", "ev"),
        P("own"),
        P("own"),
        P("own", None),
        P("own"),
        P("own"),
        P("own", None),
        P("own"),
        P("own"),
        P("own"),
        P(),
    )

    def body(ground_up, item_site, item_profile, *rest):
        n = lax.axis_size("own")
        items, cols = ground_up.shape
        sites, pol = rest[2].shape[0], rest[5].shape[0]
        prog = rest[6].shape[0]
        fits = cols % (n * LANES) == 0 and items % LANES == 0 and sites == LANES
        fits = fits and 2 * pol <= LANES and pol % 16 == 0 and prog <= 8
        fits = fits and n % 4 == 0 and n & (n - 1) == 0 and 3 * n <= LANES and 3 * items <= LANES * (LANES - 6)
        return (exchange if fits else shards)(ground_up, item_site, item_profile, *rest)

    return jax.shard_map(
        body,
        mesh=mesh,
        in_specs=placed,
        out_specs=(P("own", "ev"), P("own", "ev")),
        check_vma=False,
    )
```

profile of v0, /device:TPU:0, one launch (start us, length us, event | category | flops | bytes accessed | tf_op | source)
XLA Modules:
  0.0 32.0 jit_solution(10194723791393277871)
XLA Ops:
  0.6 30.1 %loss_terms.1 = (bf16[64,2048]{1,0:T(8,128)(2,1)S(1)}, f32[2,2048]{1,0:T(2,128)S(1)}) custom-call(bf16[512,2048]{1,0:T(8,128)(2,1)} %ground.1, s32[4,128]{1,0:T(4,128)} %bitcast.11, s32[4,128]{1,0:T(4,128)} %bitcast.12, s32[1,128]{1,0:T(1,128)} %bitcast.13, s32[1,128]{1,0:T(1,128)} %bitcast.14, s32[1,128]{1,0:T(1,128)} %bitcast.15, s32[1,64]{1,0:T(1,128)} %bitcast.16, ...), custom_call_target="tpu_custom_call" | custom-call | tf_op jit(solution)/shard_map/loss_terms/pallas_call | solution.py:353
  30.7 0.7 %copy.15 = bf16[64,2048]{1,0:T(8,128)(2,1)} copy(bf16[64,2048]{1,0:T(8,128)(2,1)S(1)} %get-tuple-element.2) | data formatting | bytes 524288
  31.4 0.6 %copy.16 = f32[2,2048]{1,0:T(2,128)} copy(f32[2,2048]{1,0:T(2,128)S(1)} %get-tuple-element.3) | data formatting | bytes 32768
where the time goes:
time: 32.2 us; the launch traced here: 32 us
  Pallas kernels  30.1 us (93%)
  local copies, waits for them, and re-layouts  1.31 us (4%)
  between operations  0.64 us (2%)
    pallas_call x1, Pallas kernels, exchange(): pl.pallas_call(functools.partial(kernel, n, pol, prog), out_shape=(pltpu....  30.1 us
    unnamed x2, local copies, waits for them, and re-layouts  1.31 us

commit v1 on v0

v1 whole, which is shorter than its diff:
```python
import functools

import jax
import jax.numpy as jnp
from jax import lax
from jax.experimental import pallas as pl
from jax.experimental.pallas import tpu as pltpu
from jax.sharding import PartitionSpec as P

LANES = 128
SMALL = 10
f32 = jnp.float32
bf16 = jnp.bfloat16


def terms(x, deduct, ceiling, portion):
    return portion * jnp.minimum(jnp.maximum(x - deduct, 0.0), ceiling)


def mixed(a, b, n):
    d, bit = 0, 1
    while bit < n:
        d = d + bit * lax.rem(lax.div(a, bit) + lax.div(b, bit), 2)
        bit *= 2
    return d


def kernel(
    n,
    pol,
    prog,
    ground,
    *refs,
):
    small_in, refs = refs[:SMALL], refs[SMALL:]
    policy_out, program_out = refs[:2]
    (
        item_rows,
        site_rows,
        policy_rows,
        program_row,
        table,
        chunks,
        ids,
        square,
        item_terms,
        site_terms,
        policy_terms,
        program_terms,
        grouping,
        meta,
        near_send,
        near_recv,
        full_send,
        full_recv,
        part_send,
        part_recv,
        near_acc,
        near_losses,
        full_losses,
        full_policy,
        program_send,
        program_recv,
        marks,
        picks,
        small_sem,
        load_sem,
        part_rs,
        sends,
        recvs,
    ) = refs[2:]
    me = lax.axis_index("own")
    team = n // 2
    side = lax.div(me, team)
    seat = lax.rem(me, team)
    base = side * team
    other = (1 - side) * team
    mate = other + seat
    items = ground.shape[0]
    blocks = items // LANES
    sites = near_send.shape[1]
    width = near_send.shape[2]
    wide = 2 * width
    rows = team * pol
    META, NEAR, FULL, PART, NEAR_POLICY, FULL_POLICY, PROGRAM = range(7)

    def turn(i):
        return mixed(seat, lax.rem(i + 1, team), team)

    barrier = pltpu.get_barrier_semaphore()

    def greet(k, c):
        pl.semaphore_signal(barrier, inc=1, device_id={"own": lax.rem(me + k, n)})
        return c

    homes = (
        [item_rows.at[pl.ds(i * blocks, blocks), :] for i in range(2)]
        + [site_rows.at[pl.ds(i, 1), :] for i in range(3)]
        + [policy_rows.at[pl.ds(i, 1), :] for i in range(3)]
        + [program_row, table]
    )
    for i, (src, dst) in enumerate(zip(small_in, homes)):
        pltpu.make_async_copy(src, dst, small_sem.at[(0, 0, 1, 1, 1, 2, 2, 2, 3, 4)[i]]).start()

    lax.fori_loop(1, n, greet, 0)

    def load(i):
        return pltpu.make_async_copy(
            ground.at[:, pl.ds(pl.multiple_of(turn(i) * wide, wide), wide)],
            chunks.at[i],
            load_sem.at[i],
        )

    def start_load(i, c):
        load(i).start()
        return c

    lax.fori_loop(0, team, start_load, 0)
    with jax.named_scope("small"):
        for i, whole in enumerate((item_rows, site_rows, policy_rows, program_row, table)):
            pltpu.make_async_copy(whole, whole, small_sem.at[i]).wait()

    square[...] = jnp.zeros_like(square)
    for t in range(3):
        square[4 * t : 4 * t + 4, :] = table[t]
    columns = square[...].T
    rows_iota = lax.broadcasted_iota(jnp.int32, (LANES, LANES), 0)

    def look(profile_row, level):
        pick = rows_iota == profile_row
        return [
            jnp.sum(
                jnp.where(pick, columns[:, 4 * t + level : 4 * t + level + 1], 0.0),
                axis=0,
                keepdims=True,
            )
            for t in range(3)
        ]

    with jax.named_scope("prep"):
        ids[...] = jnp.zeros_like(ids)
        ids[0:1, 0:pol] = policy_rows[2:3, :]
        ids[0:1, pol : 2 * pol] = policy_rows[0:1, :] * prog + policy_rows[1:2, :]
        ids[1:2, 0:prog] = program_row[...]
        meta[me] = jnp.concatenate([site_rows[0:1, :] * pol + site_rows[1:2, :], ids[0:1, :]], axis=0)

        for b in range(blocks):
            grouping[:, b * LANES : (b + 1) * LANES] = (rows_iota == item_rows[b : b + 1, :]).astype(bf16)
            for t, row in enumerate(look(item_rows[blocks + b : blocks + b + 1, :], 0)):
                square[3 * b + t : 3 * b + t + 1, :] = row
        for t, row in enumerate(look(site_rows[2:3, :], 1)):
            square[3 * blocks + t : 3 * blocks + t + 1, :] = row
        for t, row in enumerate(look(ids[1:2, :], 3)):
            square[3 * blocks + 3 + t : 3 * blocks + 4 + t, :] = row
        flipped = square[...].T
        for t in range(3):
            for b in range(blocks):
                item_terms[t, b * LANES : (b + 1) * LANES, :] = jnp.broadcast_to(
                    flipped[:, 3 * b + t : 3 * b + t + 1], (LANES, LANES)
                )
            program_terms[t] = jnp.broadcast_to(
                flipped[0:prog, 3 * blocks + 3 + t : 3 * blocks + 4 + t], (prog, LANES)
            )
            site_terms[t] = jnp.broadcast_to(
                flipped[:, 3 * blocks + t : 3 * blocks + t + 1], (LANES, LANES)
            )

    def remote(kind, src, dst, d):
        return pltpu.make_async_remote_copy(src, dst, sends.at[kind], recvs.at[kind], device_id={"own": d})

    def columns_of(block):
        return pl.ds(pl.multiple_of(block * width, width), width)

    def rows_of(q, count):
        return pl.ds(pl.multiple_of(q * count, count), count)

    def meta_copy(d):
        return remote(META, meta.at[me], meta.at[me], d)

    def near_copy(g):
        return remote(NEAR, near_send.at[g], near_recv.at[seat], base + g)

    def full_copy(d):
        return remote(FULL, full_send.at[d], full_recv.at[me], d)

    def part_copy(q):
        return pltpu.make_async_remote_copy(
            part_send.at[q], part_recv.at[q], sends.at[PART], part_rs.at[q], device_id={"own": mate}
        )

    def near_policy_copy(q):
        return remote(
            NEAR_POLICY, near_losses.at[rows_of(q, pol), :], policy_out.at[:, columns_of(2 * seat)], base + q
        )

    def full_policy_copy(d):
        return remote(FULL_POLICY, full_losses.at[d], full_policy.at[me], d)

    def program_copy(d):
        return remote(PROGRAM, program_send.at[d], program_recv.at[me], d)

    def bulk(kind, ref):
        return remote(kind, ref, ref, me)

    def others(fn):
        def step(k, c):
            fn(mixed(me, n - k, n))
            return c

        lax.fori_loop(1, n, step, 0)

    def loop(start, stop, fn):
        def step(i, c):
            fn(i)
            return c

        lax.fori_loop(start, stop, step, 0)

    def spread_of(refs_terms, at, count):
        return [jnp.concatenate([refs_terms[t, at, :]] * count, axis=1) for t in range(3)]

    every = slice(None)
    low_half = lax.broadcasted_iota(jnp.int32, (sites // 2, width), 1) < width // 2

    def swap(x):
        return pltpu.roll(x, width // 2, x.ndim - 1)

    def site_losses(i):
        load(i).wait()
        g = turn(i)
        covered = terms(chunks[i].astype(f32), *spread_of(item_terms, every, wide // LANES)).astype(bf16)
        gross = jnp.dot(grouping[...], covered, preferred_element_type=f32)
        net = terms(gross, *spread_of(site_terms, every, wide // LANES))
        near = net[:, :width].astype(bf16)
        top, bottom = net[: sites // 2, width:], net[sites // 2 :, width:]
        left = jnp.where(low_half, top, swap(bottom)).astype(bf16)
        right = jnp.where(low_half, swap(top), bottom).astype(bf16)
        ours = jnp.where(side == 0, left, right)
        theirs = jnp.where(side == 0, right, left)
        full_send[other + g] = theirs

        @pl.when(g == seat)
        def _():
            near_recv[seat] = near
            full_recv[me] = ours

        @pl.when(g != seat)
        def _():
            near_send[g] = near
            full_send[base + g] = ours

    lag = team // 2

    def send_near(i):
        near_copy(turn(i)).start()

    def send_cross(i):
        full_copy(other + turn(i)).start()

    with jax.named_scope("first"):
        site_losses(0)
    with jax.named_scope("bar"):
        pl.semaphore_wait(barrier, n - 1)
    with jax.named_scope("sites"):
        others(lambda d: meta_copy(d).start())

        def near_step(i):
            site_losses(i)
            send_near(i)

        def mixed_step(i):
            site_losses(i)
            send_near(i)
            send_cross(i - lag)

        send_near(0)
        loop(1, lag, near_step)
        loop(lag, team - 1, mixed_step)
        site_losses(team - 1)
        loop(lag - 1, team, send_cross)
        loop(0, team - 1, lambda i: full_copy(base + turn(i)).start())
    with jax.named_scope("metawait"):
        bulk(META, meta.at[pl.ds(0, n - 1)]).wait_recv()

    policy_iota = lax.broadcasted_iota(jnp.int32, (n * pol, sites), 0)
    program_iota = lax.broadcasted_iota(jnp.int32, (n * prog, pol), 0)

    def learn(start):
        for o in range(team):
            for t, row in enumerate(look(meta[start + o][1:2, :], 2)):
                square[3 * o + t : 3 * o + t + 1, :] = row
        turned = square[...].T
        for o in range(team):
            for t in range(3):
                lane = 3 * o + t
                policy_terms[t, rows_of(start + o, pol), :] = jnp.broadcast_to(
                    turned[0:pol, lane : lane + 1], (pol, LANES)
                )
        which = lax.div(start, team)
        marks[which] = jnp.concatenate(
            [(program_iota == meta[start + o][1:2, pol : 2 * pol]).astype(bf16) for o in range(team)], axis=1
        )
        for o in range(team):
            picks[which, :, o * sites : (o + 1) * sites] = (policy_iota == meta[start + o][0:1, :]).astype(bf16)

    with jax.named_scope("learn"):
        learn(base)
    with jax.named_scope("nearwait"):
        bulk(NEAR, near_recv.at[pl.ds(0, team - 1)]).wait_recv()
    ours_at, theirs_at = (pl.ds(pl.multiple_of(h * pol, rows), rows) for h in (base, other))

    def near_sum(at):
        return jnp.dot(
            picks[side, at, :], near_recv[...].reshape(team * sites, width), preferred_element_type=f32
        )

    with jax.named_scope("nearsum"):
        part_send[...] = near_sum(theirs_at).astype(bf16).reshape(team, pol, width)
        loop(0, team, lambda i: part_copy(turn(i)).start())
    with jax.named_scope("nearsum2"):
        near_acc[...] = near_sum(ours_at)
    with jax.named_scope("learn2"):
        learn(other)
    with jax.named_scope("fullwait"):
        bulk(FULL, full_recv.at[pl.ds(0, n - 1)]).wait_recv()
    with jax.named_scope("fullsum"):

        def unpacked(k):
            packed = full_recv[k * team : (k + 1) * team]
            return jnp.concatenate([packed, swap(packed)], axis=1).reshape(team * sites, width)

        total = jnp.dot(picks[0], unpacked(0), preferred_element_type=f32) + jnp.dot(
            picks[1], unpacked(1), preferred_element_type=f32
        )
        loss = terms(total, *spread_of(policy_terms, every, width // LANES))
        split = loss.reshape(n, 2, pol // 2, width)
        mask = lax.broadcasted_iota(jnp.int32, (n, pol // 2, width), 2) < width // 2
        full_losses[...] = jnp.where(mask, split[:, 0], swap(split[:, 1])).astype(bf16)
        others(lambda d: full_policy_copy(d).start())
        full_policy[me] = full_losses[me]
        loss = loss.astype(bf16)
        gross = jnp.dot(marks[0], loss[0:rows], preferred_element_type=f32) + jnp.dot(
            marks[1], loss[rows : 2 * rows], preferred_element_type=f32
        )
        for o in range(n):
            program_send[o, 1] = gross[o * prog : (o + 1) * prog, :]

    def close(i):
        q = turn(i)
        part_copy(q).wait_recv()
        at = rows_of(base + q, pol)
        gross = near_acc[rows_of(q, pol), :] + part_recv[q].astype(f32)
        loss = terms(gross, *spread_of(policy_terms, at, width // LANES)).astype(bf16)
        near_losses[rows_of(q, pol), :] = loss

        @pl.when(q != seat)
        def _():
            near_policy_copy(q).start()

        @pl.when(q == seat)
        def _():
            policy_out[:, columns_of(2 * seat)] = loss

    with jax.named_scope("close"):
        loop(0, team, close)
    with jax.named_scope("progsend"):
        near_gross = jnp.dot(marks[side], near_losses[...], preferred_element_type=f32)
        for o in range(n):
            program_send[o, 0] = near_gross[o * prog : (o + 1) * prog, :]
        others(lambda d: program_copy(d).start())
        program_recv[me] = program_send[me]
    with jax.named_scope("fpolwait"):
        bulk(FULL_POLICY, full_policy.at[pl.ds(0, n - 1)]).wait_recv()
        low = lax.broadcasted_iota(jnp.int32, (pol // 2, width), 1) < width // 2
        for g in range(team):
            left, right = full_policy[g].astype(f32), full_policy[team + g].astype(f32)
            at = slice((2 * g + 1) * width, (2 * g + 2) * width)
            policy_out[: pol // 2, at] = jnp.where(low, left, swap(right)).astype(bf16)
            policy_out[pol // 2 :, at] = jnp.where(low, swap(left), right).astype(bf16)
    with jax.named_scope("sent"):
        bulk(META, meta.at[pl.ds(0, n - 1)]).wait_send()
        bulk(NEAR, near_send.at[pl.ds(0, team - 1)]).wait_send()
        bulk(FULL, full_send.at[pl.ds(0, n - 1)]).wait_send()
        bulk(PART, part_send).wait_send()
        bulk(NEAR_POLICY, near_losses.at[pl.ds(0, rows - pol), :]).wait_send()
        bulk(FULL_POLICY, full_losses.at[pl.ds(0, n - 1)]).wait_send()
        bulk(PROGRAM, program_send.at[pl.ds(0, n - 1)]).wait_send()
    with jax.named_scope("npolwait"):
        bulk(NEAR_POLICY, near_losses.at[pl.ds(0, rows - pol), :]).wait_recv()
    with jax.named_scope("progwait"):
        bulk(PROGRAM, program_recv.at[pl.ds(0, n - 1)]).wait_recv()
    with jax.named_scope("tail"):
        spread = spread_of(program_terms, every, width // LANES)
        low = lax.broadcasted_iota(jnp.int32, (prog, width), 1) < width // 2
        for g in range(team):
            near = program_recv[g, 0] + program_recv[team + g, 0]
            full = jnp.where(low, program_recv[g, 1], swap(program_recv[team + g, 1]))
            at = 2 * g * width
            program_out[:, at : at + width] = terms(near, *spread)
            program_out[:, at + width : at + 2 * width] = terms(full, *spread)


def exchange(
    ground_up,
    item_site,
    item_profile,
    site_owner,
    site_slot,
    site_profile,
    policy_owner,
    policy_slot,
    policy_profile,
    program_profile,
    term_table,
):
    n = lax.axis_size("own")
    items, cols = ground_up.shape
    sites = site_profile.shape[0]
    pol = policy_profile.shape[0]
    prog = program_profile.shape[0]
    width = cols // n
    team = n // 2

    def row(v):
        return v.reshape(-1, min(v.size, LANES))

    inputs = [
        row(v)
        for v in (
            item_site,
            item_profile,
            site_owner,
            site_slot,
            site_profile,
            policy_owner,
            policy_slot,
            policy_profile,
            program_profile,
        )
    ] + [term_table.transpose(1, 0, 2)]
    vmemspec = pl.BlockSpec(memory_space=pltpu.VMEM)
    anyspec = pl.BlockSpec(memory_space=pl.ANY)
    dma = pltpu.SemaphoreType.DMA
    return pl.pallas_call(
        functools.partial(kernel, n, pol, prog),
        out_shape=(
            pltpu.VMEM((pol, cols), bf16),
            pltpu.VMEM((prog, cols), f32),
        ),
        in_specs=[anyspec] * (1 + SMALL),
        out_specs=(vmemspec, vmemspec),
        scratch_shapes=[
            pltpu.VMEM((2 * (items // LANES), LANES), jnp.int32),
            pltpu.VMEM((3, sites), jnp.int32),
            pltpu.VMEM((3, pol), jnp.int32),
            pltpu.VMEM((1, prog), jnp.int32),
            pltpu.VMEM(inputs[-1].shape, f32),
            pltpu.VMEM((team, items, 2 * width), bf16),
            pltpu.VMEM((8, LANES), jnp.int32),
            pltpu.VMEM((LANES, LANES), f32),
            pltpu.VMEM((3, items, LANES), f32),
            pltpu.VMEM((3, sites, LANES), f32),
            pltpu.VMEM((3, n * pol, LANES), f32),
            pltpu.VMEM((3, prog, LANES), f32),
            pltpu.VMEM((sites, items), bf16),
            pltpu.VMEM((n, 2, LANES), jnp.int32),
            pltpu.VMEM((team, sites, width), bf16),
            pltpu.VMEM((team, sites, width), bf16),
            pltpu.VMEM((n, sites // 2, width), bf16),
            pltpu.VMEM((n, sites // 2, width), bf16),
            pltpu.VMEM((team, pol, width), bf16),
            pltpu.VMEM((team, pol, width), bf16),
            pltpu.VMEM((team * pol, width), f32),
            pltpu.VMEM((team * pol, width), bf16),
            pltpu.VMEM((n, pol // 2, width), bf16),
            pltpu.VMEM((n, pol // 2, width), bf16),
            pltpu.VMEM((n, 2, prog, width), f32),
            pltpu.VMEM((n, 2, prog, width), f32),
            pltpu.VMEM((2, n * prog, team * pol), bf16),
            pltpu.VMEM((2, n * pol, team * sites), bf16),
            dma((5,)),
            dma((team,)),
            dma((team,)),
            dma((7,)),
            dma((7,)),
        ],
        compiler_params=pltpu.CompilerParams(collective_id=0, has_side_effects=True),
        name="loss_terms",
    )(ground_up, *inputs)


def apply_terms(gross_loss, terms_table, tier_index, profile):
    profile_iota = jnp.arange(terms_table.shape[2], dtype=jnp.int32)
    picker = profile[:, None] == profile_iota[None, :]
    deduct = jnp.sum(jnp.where(picker, terms_table[tier_index, 0][None, :], 0.0), axis=1)[:, None]
    ceiling = jnp.sum(jnp.where(picker, terms_table[tier_index, 1][None, :], 0.0), axis=1)[:, None]
    portion = jnp.sum(jnp.where(picker, terms_table[tier_index, 2][None, :], 0.0), axis=1)[:, None]
    return portion * jnp.minimum(jnp.maximum(gross_loss - deduct, 0.0), ceiling)


def pack_rows(values, target_dev, inner_slot, owners, capacity):
    member = (target_dev[:, None] == jnp.arange(owners, dtype=jnp.int32)[None, :]).astype(jnp.int32)
    before = jnp.cumsum(member, axis=0) - member
    position = jnp.sum(before * member, axis=1)
    target = target_dev * capacity + position
    placer = jnp.arange(owners * capacity, dtype=jnp.int32)[:, None] == target[None, :]
    packed = jnp.dot(
        placer.astype(jnp.bfloat16), values, preferred_element_type=jnp.float32
    ).astype(jnp.bfloat16)
    labels = jnp.sum(jnp.where(placer, (inner_slot + 1)[None, :], 0), axis=1) - 1
    return (
        packed.reshape(owners, capacity, values.shape[1]),
        labels.astype(jnp.bfloat16).reshape(owners, capacity),
    )


def sum_rows(received, labels, slot_count):
    flattened = received.reshape(-1, received.shape[2])
    slot_marks = labels.reshape(-1).astype(jnp.int32)
    picker = (jnp.arange(slot_count, dtype=jnp.int32)[:, None] == slot_marks[None, :]).astype(
        jnp.bfloat16
    )
    return jnp.dot(picker, flattened, preferred_element_type=jnp.float32)


def shards(
    ground_up,
    item_site,
    item_profile,
    site_owner,
    site_slot,
    site_profile,
    policy_owner,
    policy_slot,
    policy_profile,
    program_profile,
    term_table,
):
    owners = lax.axis_size("own")
    covered = apply_terms(ground_up.astype(jnp.float32), term_table, 0, item_profile).astype(
        jnp.bfloat16
    )
    site_total = site_profile.shape[0]
    grouping = (jnp.arange(site_total, dtype=jnp.int32)[:, None] == item_site[None, :]).astype(
        jnp.bfloat16
    )
    site_gross = jnp.dot(grouping, covered, preferred_element_type=jnp.float32)
    site_net = apply_terms(site_gross, term_table, 1, site_profile).astype(jnp.bfloat16)
    capacity = 2 * site_total // owners
    packed, labels = pack_rows(site_net, site_owner[:, 0], site_slot, owners, capacity)
    arrived, arrived_labels = (
        lax.all_to_all(packed, "own", split_axis=0, concat_axis=0, tiled=True),
        lax.all_to_all(labels, "own", split_axis=0, concat_axis=0, tiled=True),
    )
    policy_total = policy_profile.shape[0]
    policy_gross = sum_rows(arrived, arrived_labels, policy_total)
    policy_loss = apply_terms(policy_gross, term_table, 2, policy_profile).astype(jnp.bfloat16)
    program_total = program_profile.shape[0]
    program_capacity = 3 * policy_total // owners
    sent_rows, sent_labels = pack_rows(
        policy_loss, policy_owner[:, 0], policy_slot, owners, program_capacity
    )
    got_rows, got_labels = (
        lax.all_to_all(sent_rows, "own", split_axis=0, concat_axis=0, tiled=True),
        lax.all_to_all(sent_labels, "own", split_axis=0, concat_axis=0, tiled=True),
    )
    program_gross = sum_rows(got_rows, got_labels, program_total)
    program_loss = apply_terms(program_gross, term_table, 3, program_profile)
    return (policy_loss, program_loss)


def solution(mesh):
    placed = (
        P("own", "ev"),
        P("own"),
        P("own"),
        P("own", None),
        P("own"),
        P("own"),
        P("own", None),
        P("own"),
        P("own"),
        P("own"),
        P(),
    )

    def body(ground_up, item_site, item_profile, *rest):
        n = lax.axis_size("own")
        items, cols = ground_up.shape
        sites, pol = rest[2].shape[0], rest[5].shape[0]
        prog = rest[6].shape[0]
        fits = cols % (n * LANES) == 0 and items % LANES == 0 and sites == LANES
        fits = fits and 2 * pol <= LANES and pol % 16 == 0 and prog <= 8
        fits = fits and n % 4 == 0 and n & (n - 1) == 0 and 3 * n <= LANES and 3 * items <= LANES * (LANES - 6)
        return (exchange if fits else shards)(ground_up, item_site, item_profile, *rest)

    return jax.shard_map(
        body,
        mesh=mesh,
        in_specs=placed,
        out_specs=(P("own", "ev"), P("own", "ev")),
        check_vma=False,
    )
```

time: 32.2 us -> 30.8 us (0.957)
  Pallas kernels: 30.1 us -> 28.7 us
    pallas_call x1, Pallas kernels: 30.1 us -> 28.7 us  [exchange(): pl.pallas_call(functools.partial(kernel, n, pol, prog), out_shape=(pltpu....]
where the time goes in v1:
time: 30.8 us; the launch traced here: 30.6 us
  Pallas kernels  28.7 us (93%)
  local copies, waits for them, and re-layouts  1.31 us (4%)
  between operations  0.64 us (2%)
    pallas_call x1, Pallas kernels, exchange(): pl.pallas_call(functools.partial(kernel, n, pol, prog), out_shape=(pltpu....  28.7 us
    unnamed x2, local copies, waits for them, and re-layouts  1.31 us

profile of v1, /device:TPU:0, one launch (start us, length us, event | category | flops | bytes accessed | tf_op | source)
XLA Modules:
  0.0 30.6 jit_solution(15159144313211188494)
XLA Ops:
  0.6 28.7 %loss_terms.1 = (bf16[64,2048]{1,0:T(8,128)(2,1)S(1)}, f32[2,2048]{1,0:T(2,128)S(1)}) custom-call(bf16[512,2048]{1,0:T(8,128)(2,1)} %ground.1, s32[4,128]{1,0:T(4,128)} %bitcast.11, s32[4,128]{1,0:T(4,128)} %bitcast.12, s32[1,128]{1,0:T(1,128)} %bitcast.13, s32[1,128]{1,0:T(1,128)} %bitcast.14, s32[1,128]{1,0:T(1,128)} %bitcast.15, s32[1,64]{1,0:T(1,128)} %bitcast.16, ...), custom_call_target="tpu_custom_call" | custom-call | tf_op jit(solution)/shard_map/loss_terms/pallas_call | solution.py:444
  29.3 0.7 %copy.15 = bf16[64,2048]{1,0:T(8,128)(2,1)} copy(bf16[64,2048]{1,0:T(8,128)(2,1)S(1)} %get-tuple-element.2) | data formatting | bytes 524288
  30.0 0.6 %copy.16 = f32[2,2048]{1,0:T(2,128)} copy(f32[2,2048]{1,0:T(2,128)S(1)} %get-tuple-element.3) | data formatting | bytes 32768

commit v2 on v1

--- a/solution.py
+++ b/solution.py
@@ -85,7 +85,9 @@
     META, NEAR, FULL, PART, NEAR_POLICY, FULL_POLICY, PROGRAM = range(7)
 
     def turn(i):
-        return mixed(seat, lax.rem(i + 1, team), team)
+        half = team // 2
+        late = lax.div(i, half)
+        return mixed(seat, (1 - late) * (i + half) + late * lax.rem(i + 1, half), team)
 
     barrier = pltpu.get_barrier_semaphore()
 
@@ -250,6 +252,7 @@
             full_send[base + g] = ours
 
     lag = team // 2
+    inner = lax.rem(lax.div(seat, lag) + side, 2)
 
     def send_near(i):
         near_copy(turn(i)).start()
@@ -257,27 +260,34 @@
     def send_cross(i):
         full_copy(other + turn(i)).start()
 
+    plane, corner = lax.div(me, 4), lax.rem(me, 4)
+    hops = plane + lax.div(corner, 2) + lax.rem(corner, 2)
+    ahead = lax.clamp(1, 13 - 3 * hops, team - 1)
     with jax.named_scope("first"):
-        site_losses(0)
+        loop(0, ahead, site_losses)
     with jax.named_scope("bar"):
         pl.semaphore_wait(barrier, n - 1)
     with jax.named_scope("sites"):
         others(lambda d: meta_copy(d).start())
 
-        def near_step(i):
+        def send(i):
+            send_near(i)
+            @pl.when(inner == 1)
+            def _():
+                send_cross(i)
+
+            @pl.when((inner == 0) & (i >= lag))
+            def _():
+                send_cross(i - lag)
+
+        def step(i):
             site_losses(i)
-            send_near(i)
-
-        def mixed_step(i):
-            site_losses(i)
-            send_near(i)
-            send_cross(i - lag)
-
-        send_near(0)
-        loop(1, lag, near_step)
-        loop(lag, team - 1, mixed_step)
+            send(i)
+
+        loop(0, ahead, send)
+        loop(ahead, team - 1, step)
         site_losses(team - 1)
-        loop(lag - 1, team, send_cross)
+        loop(lax.select(inner == 1, team - 1, lag - 1), team, send_cross)
         loop(0, team - 1, lambda i: full_copy(base + turn(i)).start())
     with jax.named_scope("metawait"):
         bulk(META, meta.at[pl.ds(0, n - 1)]).wait_recv()

time: 30.8 us -> 29.3 us (0.951)
  Pallas kernels: 28.7 us -> 27.2 us
    pallas_call x1, Pallas kernels: 28.7 us -> 27.2 us  [exchange(): pl.pallas_call(functools.partial(kernel, n, pol, prog), out_shape=(pltpu....]
where the time goes in v2:
time: 29.3 us; the launch traced here: 29.1 us
  Pallas kernels  27.2 us (93%)
  local copies, waits for them, and re-layouts  1.31 us (4%)
  between operations  0.64 us (2%)
    pallas_call x1, Pallas kernels, exchange(): pl.pallas_call(functools.partial(kernel, n, pol, prog), out_shape=(pltpu....  27.2 us
    unnamed x2, local copies, waits for them, and re-layouts  1.31 us

profile of v2, /device:TPU:0, one launch (start us, length us, event | category | flops | bytes accessed | tf_op | source)
XLA Modules:
  0.0 29.1 jit_solution(2593401694060724141)
XLA Ops:
  0.6 27.2 %loss_terms.1 = (bf16[64,2048]{1,0:T(8,128)(2,1)S(1)}, f32[2,2048]{1,0:T(2,128)S(1)}) custom-call(bf16[512,2048]{1,0:T(8,128)(2,1)} %ground.1, s32[4,128]{1,0:T(4,128)} %bitcast.11, s32[4,128]{1,0:T(4,128)} %bitcast.12, s32[1,128]{1,0:T(1,128)} %bitcast.13, s32[1,128]{1,0:T(1,128)} %bitcast.14, s32[1,128]{1,0:T(1,128)} %bitcast.15, s32[1,64]{1,0:T(1,128)} %bitcast.16, ...), custom_call_target="tpu_custom_call" | custom-call | tf_op jit(solution)/shard_map/loss_terms/pallas_call | solution.py:454
  27.8 0.7 %copy.15 = bf16[64,2048]{1,0:T(8,128)(2,1)} copy(bf16[64,2048]{1,0:T(8,128)(2,1)S(1)} %get-tuple-element.2) | data formatting | bytes 524288
  28.5 0.6 %copy.16 = f32[2,2048]{1,0:T(2,128)} copy(f32[2,2048]{1,0:T(2,128)S(1)} %get-tuple-element.3) | data formatting | bytes 32768

commit v3 on v2

--- a/solution.py
+++ b/solution.py
@@ -185,9 +185,12 @@
     def full_copy(d):
         return remote(FULL, full_send.at[d], full_recv.at[me], d)
 
+    chunk = team // 2
+
     def part_copy(q):
+        at = pl.ds(q * chunk, chunk)
         return pltpu.make_async_remote_copy(
-            part_send.at[q], part_recv.at[q], sends.at[PART], part_rs.at[q], device_id={"own": mate}
+            part_send.at[at], part_recv.at[at], sends.at[PART], part_rs.at[q], device_id={"own": mate}
         )
 
     def near_policy_copy(q):
@@ -326,7 +329,7 @@
 
     with jax.named_scope("nearsum"):
         part_send[...] = near_sum(theirs_at).astype(bf16).reshape(team, pol, width)
-        loop(0, team, lambda i: part_copy(turn(i)).start())
+        loop(0, 2, lambda i: part_copy(lax.rem(i + lax.div(seat, chunk), 2)).start())
     with jax.named_scope("nearsum2"):
         near_acc[...] = near_sum(ours_at)
     with jax.named_scope("learn2"):
@@ -356,8 +359,12 @@
             program_send[o, 1] = gross[o * prog : (o + 1) * prog, :]
 
     def close(i):
-        q = turn(i)
-        part_copy(q).wait_recv()
+        q = lax.rem(i + lax.div(seat, chunk) * chunk, team)
+
+        @pl.when(lax.rem(i, chunk) == 0)
+        def _():
+            part_copy(lax.div(q, chunk)).wait_recv()
+
         at = rows_of(base + q, pol)
         gross = near_acc[rows_of(q, pol), :] + part_recv[q].astype(f32)
         loss = terms(gross, *spread_of(policy_terms, at, width // LANES)).astype(bf16)
@@ -410,6 +417,17 @@
             program_out[:, at + width : at + 2 * width] = terms(full, *spread)
 
 
+def store(policy, program, policy_out, program_out, sems):
+    copies = [
+        pltpu.make_async_copy(policy, policy_out, sems.at[0]),
+        pltpu.make_async_copy(program, program_out, sems.at[1]),
+    ]
+    for copy in copies:
+        copy.start()
+    for copy in copies:
+        copy.wait()
+
+
 def exchange(
     ground_up,
     item_site,
@@ -451,7 +469,7 @@
     vmemspec = pl.BlockSpec(memory_space=pltpu.VMEM)
     anyspec = pl.BlockSpec(memory_space=pl.ANY)
     dma = pltpu.SemaphoreType.DMA
-    return pl.pallas_call(
+    held = pl.pallas_call(
         functools.partial(kernel, n, pol, prog),
         out_shape=(
             pltpu.VMEM((pol, cols), bf16),
@@ -490,13 +508,22 @@
             pltpu.VMEM((2, n * pol, team * sites), bf16),
             dma((5,)),
             dma((team,)),
-            dma((team,)),
+            dma((2,)),
             dma((7,)),
             dma((7,)),
         ],
         compiler_params=pltpu.CompilerParams(collective_id=0, has_side_effects=True),
         name="loss_terms",
     )(ground_up, *inputs)
+    held = [pltpu.with_memory_space_constraint(v, pltpu.VMEM) for v in held]
+    return pl.pallas_call(
+        store,
+        out_shape=tuple(jax.ShapeDtypeStruct(v.shape, v.dtype) for v in held),
+        in_specs=[vmemspec] * 2,
+        out_specs=(anyspec, anyspec),
+        scratch_shapes=[dma((2,))],
+        name="store_losses",
+    )(*held)
 
 
 def apply_terms(gross_loss, terms_table, tier_index, profile):

time: 29.3 us -> 28.7 us (0.980)
  local copies, waits for them, and re-layouts: 1.31 us -> 0 us
  Pallas kernels: 27.2 us -> 27.9 us
    unnamed x2 -> x0, local copies, waits for them, and re-layouts: 1.31 us -> none
    pallas_call x0 -> x1, Pallas kernels: none -> 0.72 us  [exchange(): pl.pallas_call(store, out_shape=tuple((jax.ShapeDtypeStruct(v.shape, v.dt...]
where the time goes in v3:
time: 28.7 us; the launch traced here: 28.5 us
  Pallas kernels  27.9 us (97%)
  between operations  0.64 us (2%)
    pallas_call x1, Pallas kernels, exchange(): pl.pallas_call(functools.partial(kernel, n, pol, prog), out_shape=(pltpu....  27.1 us
    pallas_call x1, Pallas kernels, exchange(): pl.pallas_call(store, out_shape=tuple((jax.ShapeDtypeStruct(v.shape, v.dt...  0.72 us

profile of v3, /device:TPU:0, one launch (start us, length us, event | category | flops | bytes accessed | tf_op | source)
XLA Modules:
  0.0 28.5 jit_solution(1883549281466697927)
XLA Ops:
  0.6 27.1 %loss_terms.1 = (bf16[64,2048]{1,0:T(8,128)(2,1)S(1)}, f32[2,2048]{1,0:T(2,128)S(1)}) custom-call(bf16[512,2048]{1,0:T(8,128)(2,1)} %ground.1, s32[4,128]{1,0:T(4,128)} %bitcast.11, s32[4,128]{1,0:T(4,128)} %bitcast.12, s32[1,128]{1,0:T(1,128)} %bitcast.13, s32[1,128]{1,0:T(1,128)} %bitcast.14, s32[1,128]{1,0:T(1,128)} %bitcast.15, s32[1,64]{1,0:T(1,128)} %bitcast.16, ...), custom_call_target="tpu_custom_call" | custom-call | tf_op jit(solution)/shard_map/loss_terms/pallas_call | solution.py:472
  27.8 0.7 %store_losses.1 = (bf16[64,2048]{1,0:T(8,128)(2,1)}, f32[2,2048]{1,0:T(2,128)}) custom-call(bf16[64,2048]{1,0:T(8,128)(2,1)S(1)} %get-tuple-element.4.policy, f32[2,2048]{1,0:T(2,128)S(1)} %get-tuple-element.5.program), custom_call_target="tpu_custom_call" | custom-call | tf_op jit(solution)/shard_map/store_losses/pallas_call | solution.py:519

commit v4 on v3

--- a/solution.py
+++ b/solution.py
@@ -140,29 +140,18 @@
         ]
 
     with jax.named_scope("prep"):
-        ids[...] = jnp.zeros_like(ids)
-        ids[0:1, 0:pol] = policy_rows[2:3, :]
-        ids[0:1, pol : 2 * pol] = policy_rows[0:1, :] * prog + policy_rows[1:2, :]
-        ids[1:2, 0:prog] = program_row[...]
-        meta[me] = jnp.concatenate([site_rows[0:1, :] * pol + site_rows[1:2, :], ids[0:1, :]], axis=0)
-
         for b in range(blocks):
             grouping[:, b * LANES : (b + 1) * LANES] = (rows_iota == item_rows[b : b + 1, :]).astype(bf16)
             for t, row in enumerate(look(item_rows[blocks + b : blocks + b + 1, :], 0)):
                 square[3 * b + t : 3 * b + t + 1, :] = row
         for t, row in enumerate(look(site_rows[2:3, :], 1)):
             square[3 * blocks + t : 3 * blocks + t + 1, :] = row
-        for t, row in enumerate(look(ids[1:2, :], 3)):
-            square[3 * blocks + 3 + t : 3 * blocks + 4 + t, :] = row
         flipped = square[...].T
         for t in range(3):
             for b in range(blocks):
                 item_terms[t, b * LANES : (b + 1) * LANES, :] = jnp.broadcast_to(
                     flipped[:, 3 * b + t : 3 * b + t + 1], (LANES, LANES)
                 )
-            program_terms[t] = jnp.broadcast_to(
-                flipped[0:prog, 3 * blocks + 3 + t : 3 * blocks + 4 + t], (prog, LANES)
-            )
             site_terms[t] = jnp.broadcast_to(
                 flipped[:, 3 * blocks + t : 3 * blocks + t + 1], (LANES, LANES)
             )
@@ -213,6 +202,16 @@
             return c
 
         lax.fori_loop(1, n, step, 0)
+
+    def ascending(fn):
+        def step(d, c):
+            @pl.when(d != me)
+            def _():
+                fn(d)
+
+            return c
+
+        lax.fori_loop(0, n, step, 0)
 
     def loop(start, stop, fn):
         def step(i, c):
@@ -268,10 +267,16 @@
     ahead = lax.clamp(1, 13 - 3 * hops, team - 1)
     with jax.named_scope("first"):
         loop(0, ahead, site_losses)
+    ids[...] = jnp.zeros_like(ids)
+    ids[0:1, 0:pol] = policy_rows[2:3, :]
+    ids[0:1, pol : 2 * pol] = policy_rows[0:1, :] * prog + policy_rows[1:2, :]
+    ids[1:2, 0:prog] = program_row[...]
+    meta[me] = jnp.concatenate([site_rows[0:1, :] * pol + site_rows[1:2, :], ids[0:1, :]], axis=0)
+
     with jax.named_scope("bar"):
         pl.semaphore_wait(barrier, n - 1)
     with jax.named_scope("sites"):
-        others(lambda d: meta_copy(d).start())
+        loop(1, n, lambda k: meta_copy(lax.rem(me + k, n)).start())
 
         def send(i):
             send_near(i)
@@ -334,6 +339,11 @@
         near_acc[...] = near_sum(ours_at)
     with jax.named_scope("learn2"):
         learn(other)
+        for t, row in enumerate(look(ids[1:2, :], 3)):
+            square[t : t + 1, :] = row
+        tilted = square[...].T
+        for t in range(3):
+            program_terms[t] = jnp.broadcast_to(tilted[0:prog, t : t + 1], (prog, LANES))
     with jax.named_scope("fullwait"):
         bulk(FULL, full_recv.at[pl.ds(0, n - 1)]).wait_recv()
     with jax.named_scope("fullsum"):
@@ -349,7 +359,12 @@
         split = loss.reshape(n, 2, pol // 2, width)
         mask = lax.broadcasted_iota(jnp.int32, (n, pol // 2, width), 2) < width // 2
         full_losses[...] = jnp.where(mask, split[:, 0], swap(split[:, 1])).astype(bf16)
-        others(lambda d: full_policy_copy(d).start())
+        core = lax.axis_index("ev")
+
+        @pl.when(core == 0)
+        def _():
+            ascending(lambda d: full_policy_copy(d).start())
+
         full_policy[me] = full_losses[me]
         loss = loss.astype(bf16)
         gross = jnp.dot(marks[0], loss[0:rows], preferred_element_type=f32) + jnp.dot(
@@ -380,11 +395,16 @@
 
     with jax.named_scope("close"):
         loop(0, team, close)
+
+        @pl.when(core != 0)
+        def _():
+            ascending(lambda d: full_policy_copy(d).start())
+
     with jax.named_scope("progsend"):
         near_gross = jnp.dot(marks[side], near_losses[...], preferred_element_type=f32)
         for o in range(n):
             program_send[o, 0] = near_gross[o * prog : (o + 1) * prog, :]
-        others(lambda d: program_copy(d).start())
+        ascending(lambda d: program_copy(d).start())
         program_recv[me] = program_send[me]
     with jax.named_scope("fpolwait"):
         bulk(FULL_POLICY, full_policy.at[pl.ds(0, n - 1)]).wait_recv()

time: 28.7 us -> 28.3 us (0.986)
  Pallas kernels: 27.9 us -> 27.5 us
    pallas_call x1, Pallas kernels: 27.1 us -> 26.8 us  [exchange(): pl.pallas_call(functools.partial(kernel, n, pol, prog), out_shape=(pltpu....]
where the time goes in v4:
time: 28.3 us; the launch traced here: 28.1 us
  Pallas kernels  27.5 us (97%)
  between operations  0.64 us (2%)
    pallas_call x1, Pallas kernels, exchange(): pl.pallas_call(functools.partial(kernel, n, pol, prog), out_shape=(pltpu....  26.8 us
    pallas_call x1, Pallas kernels, exchange(): pl.pallas_call(store, out_shape=tuple((jax.ShapeDtypeStruct(v.shape, v.dt...  0.72 us

profile of v4, /device:TPU:0, one launch (start us, length us, event | category | flops | bytes accessed | tf_op | source)
XLA Modules:
  0.0 28.1 jit_solution(8430827066691015202)
XLA Ops:
  0.6 26.8 %loss_terms.1 = (bf16[64,2048]{1,0:T(8,128)(2,1)S(1)}, f32[2,2048]{1,0:T(2,128)S(1)}) custom-call(bf16[512,2048]{1,0:T(8,128)(2,1)} %ground.1, s32[4,128]{1,0:T(4,128)} %bitcast.11, s32[4,128]{1,0:T(4,128)} %bitcast.12, s32[1,128]{1,0:T(1,128)} %bitcast.13, s32[1,128]{1,0:T(1,128)} %bitcast.14, s32[1,128]{1,0:T(1,128)} %bitcast.15, s32[1,64]{1,0:T(1,128)} %bitcast.16, ...), custom_call_target="tpu_custom_call" | custom-call | tf_op jit(solution)/shard_map/loss_terms/pallas_call | solution.py:492
  27.4 0.7 %store_losses.1 = (bf16[64,2048]{1,0:T(8,128)(2,1)}, f32[2,2048]{1,0:T(2,128)}) custom-call(bf16[64,2048]{1,0:T(8,128)(2,1)S(1)} %get-tuple-element.4.policy, f32[2,2048]{1,0:T(2,128)S(1)} %get-tuple-element.5.program), custom_call_target="tpu_custom_call" | custom-call | tf_op jit(solution)/shard_map/store_losses/pallas_call | solution.py:539

commit v5 on v4

--- a/solution.py
+++ b/solution.py
@@ -253,7 +253,7 @@
             near_send[g] = near
             full_send[base + g] = ours
 
-    lag = team // 2
+    lag = team // 2 + 1
     inner = lax.rem(lax.div(seat, lag) + side, 2)
 
     def send_near(i):
@@ -295,7 +295,7 @@
         loop(0, ahead, send)
         loop(ahead, team - 1, step)
         site_losses(team - 1)
-        loop(lax.select(inner == 1, team - 1, lag - 1), team, send_cross)
+        loop(lax.select(inner == 1, team - 1, team - 1 - lag), team, send_cross)
         loop(0, team - 1, lambda i: full_copy(base + turn(i)).start())
     with jax.named_scope("metawait"):
         bulk(META, meta.at[pl.ds(0, n - 1)]).wait_recv()

time: 28.3 us -> 28.3 us (level)
  no operation moved by 1% of the time
where the time goes in v5:
time: 28.3 us; the launch traced here: 28.2 us
  Pallas kernels  27.5 us (97%)
  between operations  0.64 us (2%)
    pallas_call x1, Pallas kernels, exchange(): pl.pallas_call(functools.partial(kernel, n, pol, prog), out_shape=(pltpu....  26.8 us
    pallas_call x1, Pallas kernels, exchange(): pl.pallas_call(store, out_shape=tuple((jax.ShapeDtypeStruct(v.shape, v.dt...  0.72 us

profile of v5, /device:TPU:0, one launch (start us, length us, event | category | flops | bytes accessed | tf_op | source)
XLA Modules:
  0.0 28.2 jit_solution(2633097745288475228)
XLA Ops:
  0.6 26.8 %loss_terms.1 = (bf16[64,2048]{1,0:T(8,128)(2,1)S(1)}, f32[2,2048]{1,0:T(2,128)S(1)}) custom-call(bf16[512,2048]{1,0:T(8,128)(2,1)} %ground.1, s32[4,128]{1,0:T(4,128)} %bitcast.11, s32[4,128]{1,0:T(4,128)} %bitcast.12, s32[1,128]{1,0:T(1,128)} %bitcast.13, s32[1,128]{1,0:T(1,128)} %bitcast.14, s32[1,128]{1,0:T(1,128)} %bitcast.15, s32[1,64]{1,0:T(1,128)} %bitcast.16, ...), custom_call_target="tpu_custom_call" | custom-call | tf_op jit(solution)/shard_map/loss_terms/pallas_call | solution.py:492
  27.5 0.7 %store_losses.1 = (bf16[64,2048]{1,0:T(8,128)(2,1)}, f32[2,2048]{1,0:T(2,128)}) custom-call(bf16[64,2048]{1,0:T(8,128)(2,1)S(1)} %get-tuple-element.4.policy, f32[2,2048]{1,0:T(2,128)S(1)} %get-tuple-element.5.program), custom_call_target="tpu_custom_call" | custom-call | tf_op jit(solution)/shard_map/store_losses/pallas_call | solution.py:539
